TPU v7x, 256 devices: a whole 4x4x8 slice. The times are simulated.
256 devices in a mesh: member: 4 (over y), lat: 64 (over x, z, core).
Axes of the slice: x: 4, y: 4, z: 8, core: 2. Of those that a mesh axis runs over, the one named last changes fastest.
Arguments:
- ensemble_starting_fields: bfloat16 [4, 256, 512, 384], P('member', 'lat'), may hold values from -6 to 6
- observed: bfloat16 [256, 512, 384], P('lat'), may hold values from -6 to 6
- wave_of_slot: int32 [256], replicated, may hold values from 0 to 255, each once
- leg_forward: bfloat16 [256, 256, 256], P('lat'), may hold values from -0.375 to 0.375
- leg_inverse: bfloat16 [256, 256, 256], P('lat'), may hold values from -0.375 to 0.375
- spec_filter: float32 [2, 256, 384], replicated, may hold values from -5 to 5
- gain_first: float32 [384], replicated, may hold values from 0.5 to 1.5
- gain_second: float32 [384], replicated, may hold values from 0.5 to 1.5
- weight_in: bfloat16 [384, 768], replicated, may hold values from -0.3125 to 0.3125
- weight_out: bfloat16 [768, 384], replicated, may hold values from -0.21875 to 0.21875
Outputs:
- predicted_field: bfloat16 [4, 256, 512, 384], P('member', 'lat')
- proper_loss_slope: bfloat16 [4, 256, 512, 384], P('member', 'lat')
Inputs may be any that keep to these rules, and one draw needn't show every extreme that they name: `wave_of_slot`: every wavenumber 0 to 255 sits in exactly one slot.
All inputs are finite; a program needn't handle non-finite values.
Results may differ from a plain program's by a relative error of at most 0.013.
Values may be sent and summed in bfloat16 or wider, within the bound.
A program may use at most 64 MiB of HBM per device.

v0:
```python
import math

import jax
import jax.numpy as jnp
from jax import lax
from jax.sharding import PartitionSpec as P

EPS_NORM = 1e-05
EPS_DIST = 1e-06


def layer_norm(values, scales):
    average = jnp.mean(values, -1, keepdims=True)
    centred = values - average
    spread = jnp.mean(centred * centred, -1, keepdims=True)
    return centred * lax.rsqrt(spread + EPS_NORM) * scales


def distance(first, second):
    return jnp.sqrt(jnp.mean(jnp.square(first - second), -1, keepdims=True) + EPS_DIST)


def dft_tables(numbers, length):
    columns = jnp.arange(length, dtype=jnp.int32)
    phases = numbers[:, None] * columns[None, :] % length
    angles = phases.astype(jnp.float32) * (2.0 * math.pi / length)
    return (jnp.cos(angles), jnp.sin(angles))


def split_table(table):
    table_high = table.astype(jnp.bfloat16)
    table_low = (table - table_high.astype(jnp.float32)).astype(jnp.bfloat16)
    return (table_high, table_low)


def member_grad(own, others, target, divisor):
    pulled = jnp.zeros_like(own)
    for other in others:
        pulled = pulled + (own - other) / distance(own, other)
    return (own - target) / distance(own, target) - pulled / divisor


def local(
    ensemble_starting_fields,
    observed,
    wave_of_slot,
    leg_forward,
    leg_inverse,
    spec_filter,
    gain_first,
    gain_second,
    weight_in,
    weight_out,
):
    lat_rows = ensemble_starting_fields.shape[1]
    length = ensemble_starting_fields.shape[2]
    channels = ensemble_starting_fields.shape[3]
    waves_all = wave_of_slot.shape[0]
    slots = leg_forward.shape[0]
    degrees = leg_forward.shape[1]
    values = ensemble_starting_fields[0].astype(jnp.float32)
    normed = layer_norm(values, gain_first).astype(jnp.bfloat16)
    cosines, sines = dft_tables(wave_of_slot, length)
    fwd_table = jnp.stack([cosines / length, -sines / length], 1).reshape(2 * waves_all, length)
    fwd_high, fwd_low = split_table(fwd_table)
    analysis = jnp.einsum("kj,ljc->klc", fwd_high, normed, preferred_element_type=jnp.float32)
    analysis = analysis + jnp.einsum(
        "kj,ljc->klc", fwd_low, normed, preferred_element_type=jnp.float32
    )
    analysis = analysis.astype(jnp.bfloat16).reshape(waves_all, 2, lat_rows, channels)
    spectra = lax.all_to_all(analysis, "lat", split_axis=0, concat_axis=2, tiled=True)
    local_waves = lax.dynamic_slice_in_dim(wave_of_slot, lax.axis_index("lat") * slots, slots)
    order = jnp.arange(degrees, dtype=jnp.int32)
    retain = (order[None, :] >= local_waves[:, None]).astype(jnp.float32)[:, None, :, None]
    filt_real = spec_filter[0]
    filt_imag = spec_filter[1]
    coeffs = (
        jnp.einsum("sln,srnc->srlc", leg_forward, spectra, preferred_element_type=jnp.float32)
        * retain
    )
    real_part = coeffs[:, 0]
    imag_part = coeffs[:, 1]
    filtered = jnp.stack(
        [
            real_part * filt_real - imag_part * filt_imag,
            real_part * filt_imag + imag_part * filt_real,
        ],
        1,
    ).astype(jnp.bfloat16)
    synthesis = jnp.einsum(
        "snl,srlc->srnc", leg_inverse, filtered, preferred_element_type=jnp.float32
    )
    synthesis = synthesis.astype(jnp.bfloat16)
    returned = lax.all_to_all(synthesis, "lat", split_axis=2, concat_axis=0, tiled=True)
    returned = returned.reshape(2 * waves_all, lat_rows, channels)
    weights_m = jnp.where(wave_of_slot == 0, 1.0, 2.0).astype(jnp.float32)[:, None]
    inv_table = jnp.stack([weights_m * cosines, -weights_m * sines], 1).reshape(
        2 * waves_all, length
    )
    inv_high, inv_low = split_table(inv_table)
    spectral = jnp.einsum("kj,klc->ljc", inv_high, returned, preferred_element_type=jnp.float32)
    spectral = spectral + jnp.einsum(
        "kj,klc->ljc", inv_low, returned, preferred_element_type=jnp.float32
    )
    harmonic_damped_field = values + spectral
    normed_two = (
        layer_norm(harmonic_damped_field, gain_second)
        .astype(jnp.bfloat16)
        .reshape(lat_rows * length, channels)
    )
    hidden = jax.nn.gelu(jnp.dot(normed_two, weight_in, preferred_element_type=jnp.float32)).astype(
        jnp.bfloat16
    )
    feedforward_result = jnp.dot(hidden, weight_out, preferred_element_type=jnp.float32).reshape(
        lat_rows, length, channels
    )
    predicted_field = (harmonic_damped_field + feedforward_result).astype(jnp.bfloat16)[None]
    members = lax.axis_size("member")
    gathered_fields = lax.all_to_all(
        predicted_field, "member", split_axis=2, concat_axis=0, tiled=True
    )
    block_cols = length // members
    first_col = lax.axis_index("member") * block_cols
    target = lax.dynamic_slice_in_dim(observed, first_col, block_cols, 1).astype(jnp.float32)
    others = [gathered_fields[member_index].astype(jnp.float32) for member_index in range(members)]
    grads = [
        member_grad(others[member_index], others, target, members - 1)
        for member_index in range(members)
    ]
    grads = jnp.stack(grads, 0).astype(jnp.bfloat16)
    proper_loss_slope = lax.all_to_all(grads, "member", split_axis=0, concat_axis=2, tiled=True)
    return (predicted_field, proper_loss_slope)


def solution(mesh):
    in_specs = (
        P("member", "lat", None, None),
        P("lat", None, None),
        P(),
        P("lat", None, None),
        P("lat", None, None),
        P(),
        P(),
        P(),
        P(),
        P(),
    )
    out_specs = (P("member", "lat", None, None), P("member", "lat", None, None))
    return jax.shard_map(local, mesh=mesh, in_specs=in_specs, out_specs=out_specs, check_vma=False)
```

profile of v0, /device:TPU:2, one launch (start us, length us, event | category | flops | bytes accessed | tf_op | source)
XLA Modules:
  0.0 218.4 jit_solution(14506223349194747387)
XLA Ops:
  1.4 2.9 %broadcast_multiply_fusion.1 = (f32[256,1,512]{2,0,1:T(8,128)S(1)}, f32[256,1,512]{2,0,1:T(8,128)S(1)}, f32[256,1,512]{2,0,1:T(8,128)S(1)}, f32[256,1,512]{2,0,1:T(8,128)S(1)}) fusion(f32[256]{0:T(256)S(1)} %get-tuple-element.50, s32[256]{0:T(256)} %param.12, f32[256]{0:T(256)S(1)} %get-tuple-element.51), kind=kLoop, calls=%fused_computation.136 | loop fusion | flops 2490368 | bytes 2100224 | tf_op jit(solution)/shard_map/mul | solution.py:97
  4.3 1.3 subtract_convert_fusion.1
  6.5 1.7 copy.92
  12.7 1.2 add_convert_fusion.1
  13.9 2.4 %copy.119 = bf16[512,4,384]{2,1,0:T(4,128)(2,1)} copy(bf16[512,4,384]{2,0,1:T(8,128)(2,1)S(1)} %add_convert_fusion.1) | data formatting | bytes 3145728 | tf_op jit(solution)/shard_map/reshape | solution.py:70
  16.2 12.3 %all-to-all-start = ((bf16[256,2,4,384]{3,2,1,0:T(4,128)(2,1)}), bf16[256,2,4,384]{3,2,1,0:T(4,128)(2,1)}, u32[]{:S(2)}, u32[]{:S(2)}) async-start(bf16[256,2,4,384]{3,2,1,0:T(4,128)(2,1)} %bitcast.185), calls=%async_computation | async-start | bytes 3145728 | tf_op jit(solution)/shard_map/all_to_all | solution.py:71
  30.3 36.7 %all-to-all-done = bf16[256,2,4,384]{3,2,1,0:T(4,128)(2,1)} async-done(((bf16[256,2,4,384]{3,2,1,0:T(4,128)(2,1)}), bf16[256,2,4,384]{3,2,1,0:T(4,128)(2,1)}, u32[]{:S(2)}, u32[]{:S(2)}) %all-to-all-start) | async-done | bytes 1572896 | tf_op jit(solution)/shard_map/all_to_all | solution.py:71
  67.0 3.1 %copy.98 = bf16[4,2,64,4,384]{4,1,3,2,0:T(2,128)(2,1)S(1)} copy(bf16[4,2,64,4,384]{4,3,1,0,2:T(4,128)(2,1)} %bitcast.4) | data formatting | bytes 3145728 | tf_op jit(solution)/shard_map/all_to_all | solution.py:71
  71.9 1.8 fusion.25
  73.6 4.9 %copy.102 = bf16[4,2,256,384]{3,1,0,2:T(2,128)(2,1)} copy(bf16[4,2,256,384]{2,3,1,0:T(8,128)(2,1)} %fusion.25) | data formatting | bytes 3145728 | tf_op jit(solution)/shard_map/convert_element_type | solution.py:93
  78.5 7.7 %all-to-all-start.1 = ((bf16[4,2,256,384]{3,1,0,2:T(2,128)(2,1)}), bf16[4,2,256,384]{3,1,0,2:T(2,128)(2,1)}, u32[]{:S(2)}, u32[]{:S(2)}) async-start(bf16[4,2,256,384]{3,1,0,2:T(2,128)(2,1)} %copy.102), calls=%async_computation.1 | async-start | bytes 3145728 | tf_op jit(solution)/shard_map/all_to_all | solution.py:94
  87.0 2.4 %copy.107 = bf16[256,2,512]{2,1,0:T(2,128)(2,1)} copy(bf16[256,2,512]{2,0,1:T(8,128)(2,1)} %get-tuple-element.54) | data formatting | bytes 1048576 | tf_op jit(solution)/shard_map/convert_element_type | solution.py:32
  89.4 1.2 reshape.467
  90.6 34.0 %all-to-all-done.1 = bf16[4,2,256,384]{3,1,0,2:T(2,128)(2,1)} async-done(((bf16[4,2,256,384]{3,1,0,2:T(2,128)(2,1)}), bf16[4,2,256,384]{3,1,0,2:T(2,128)(2,1)}, u32[]{:S(2)}, u32[]{:S(2)}) %all-to-all-start.1) | async-done | bytes 1572896 | tf_op jit(solution)/shard_map/all_to_all | solution.py:94
  124.6 3.4 %copy.104 = bf16[64,4,2,4,384]{4,3,2,1,0:T(4,128)(2,1)} copy(bf16[64,4,2,4,384]{4,2,1,3,0:T(2,128)(2,1)} %bitcast.16) | data formatting | bytes 3145728 | tf_op jit(solution)/shard_map/all_to_all | solution.py:94
  128.0 3.7 %copy.106 = bf16[512,4,384]{0,2,1:T(8,128)(2,1)} copy(bf16[512,4,384]{2,1,0:T(4,128)(2,1)} %bitcast.186) | data formatting | bytes 3145728 | tf_op jit(solution)/shard_map/reshape | solution.py:95
  131.7 2.5 %fusion.88 = f32[4,384,512]{2,1,0:T(8,128)S(1)} fusion(bf16[512,4,384]{0,2,1:T(8,128)(2,1)} %copy.106, bf16[512,512,1]{1,0,2:T(8,128)(2,1)S(1)} %reshape.466), kind=kOutput, calls=%fused_computation.175 | convolution fusion | flops 805306368 | bytes 5242880 | tf_op jit(solution)/shard_map/kj,klc->ljc/dot_general | solution.py:101
  135.9 1.2 copy-done.1
  137.5 1.6 copy.109
  139.1 6.8 %fusion.15 = f32[2048,384]{1,0:T(8,128)} fusion(bf16[768,384]{1,0:T(8,128)(2,1)S(1)} %copy-done, bf16[2048,384]{1,0:T(8,128)(2,1)} %bitcast.190, bf16[384,768]{1,0:T(8,128)(2,1)S(1)} %copy-done.10), kind=kOutput, calls=%fused_computation.24 | convolution fusion | flops 2430074880 | bytes 5898240 | tf_op jit(solution)/shard_map/dot_general | solution.py:114
  145.9 3.6 %copy.110 = f32[4,512,384]{1,2,0:T(8,128)} copy(f32[4,512,384]{2,1,0:T(8,128)} %bitcast.188) | data formatting | bytes 6291456 | tf_op jit(solution)/shard_map/reshape | solution.py:114
  149.4 3.4 %fusion.19 = bf16[1,4,512,384]{2,3,1,0:T(8,128)(2,1)S(1)} fusion(f32[4,512,384]{1,2,0:T(8,128)} %copy-done.1, f32[4,512,384]{1,2,0:T(8,128)} %copy.110), kind=kLoop, calls=%fused_computation.47 | loop fusion | flops 1572864 | bytes 7864320 | tf_op jit(solution)/shard_map/broadcast_in_dim | solution.py:117
  152.8 2.2 %copy.111 = bf16[1,4,512,384]{3,1,0,2:T(4,128)(2,1)} copy(bf16[1,4,512,384]{2,3,1,0:T(8,128)(2,1)S(1)} %fusion.19) | data formatting | bytes 3145728 | tf_op jit(solution)/shard_map/broadcast_in_dim | solution.py:117
  155.0 4.6 %all-to-all-start.2 = ((bf16[1,4,512,384]{3,1,0,2:T(4,128)(2,1)}), bf16[1,4,512,384]{3,1,0,2:T(4,128)(2,1)}, u32[]{:S(2)}, u32[]{:S(2)}) async-start(bf16[1,4,512,384]{3,1,0,2:T(4,128)(2,1)} %copy.111), calls=%async_computation.2 | async-start | bytes 3145728 | tf_op jit(solution)/shard_map/all_to_all | solution.py:119
  159.6 21.8 %all-to-all-done.2 = bf16[1,4,512,384]{3,1,0,2:T(4,128)(2,1)} async-done(((bf16[1,4,512,384]{3,1,0,2:T(4,128)(2,1)}), bf16[1,4,512,384]{3,1,0,2:T(4,128)(2,1)}, u32[]{:S(2)}, u32[]{:S(2)}) %all-to-all-start.2) | async-done | bytes 1572896 | tf_op jit(solution)/shard_map/all_to_all | solution.py:119
  181.4 1.8 copy.124
  183.3 2.3 %multiply_reduce_fusion.16 = (f32[4,128]{1,0:T(4,128)S(1)}, f32[4,128]{1,0:T(4,128)S(1)}, f32[4,128]{1,0:T(4,128)S(1)}, f32[4,128]{1,0:T(4,128)S(1)}, f32[4,128]...) fusion(bf16[4,512,384]{2,1,0:T(8,128)(2,1)S(1)} %copy-done.3, ...), kind=kLoop, calls=%fused_computation.108 | loop fusion | flops 12769280 | bytes 2007044 | tf_op jit(solution)/shard_map/reduce_sum | solution.py:20
  188.5 1.4 pad_maximum_fusion
  189.9 4.3 %all-to-all-start.3 = ((bf16[4,4,128,384]{3,2,1,0:T(8,128)(2,1)}), bf16[4,4,128,384]{3,2,1,0:T(8,128)(2,1)}, u32[]{:S(2)}, u32[]{:S(2)}) async-start(bf16[4,4,128,384]{3,2,1,0:T(8,128)(2,1)} %pad_maximum_fusion), calls=%async_computation.3 | async-start | bytes 3145728 | tf_op jit(solution)/shard_map/all_to_all | solution.py:131
  194.3 1.6 copy.114
  195.8 19.8 %all-to-all-done.3 = bf16[4,4,128,384]{3,2,1,0:T(8,128)(2,1)} async-done(((bf16[4,4,128,384]{3,2,1,0:T(8,128)(2,1)}), bf16[4,4,128,384]{3,2,1,0:T(8,128)(2,1)}, u32[]{:S(2)}, u32[]{:S(2)}) %all-to-all-start.3) | async-done | bytes 1572896 | tf_op jit(solution)/shard_map/all_to_all | solution.py:131
  215.6 2.8 %copy.113 = bf16[1,4,4,128,384]{4,3,2,1,0:T(8,128)(2,1)} copy(bf16[1,4,4,128,384]{4,3,1,2,0:T(8,128)(2,1)} %bitcast.37) | data formatting | bytes 3145728 | tf_op jit(solution)/shard_map/all_to_all | solution.py:131
  (74 shorter events, 15.1 us)
Async XLA Ops:
  0.6 138.4 %copy-start = (bf16[768,384]{1,0:T(8,128)(2,1)S(1)}, bf16[768,384]{1,0:T(8,128)(2,1)}, u32[]{:S(2)}) copy-start(bf16[768,384]{1,0:T(8,128)(2,1)} %param.19) | copy-start | bytes 1769476
  8.2 1.0 copy-start.5
  9.8 1.8 copy-start.12
  11.5 1.1 copy-start.7
  16.2 12.3 %copy-start.8 = (s32[256]{0:T(256)S(1)}, s32[256]{0:T(256)}, u32[]{:S(2)}) copy-start(s32[256]{0:T(256)} %param.12) | copy-start | bytes 3076
  16.2 50.7 %all-to-all-start = ((bf16[256,2,4,384]{3,2,1,0:T(4,128)(2,1)}), bf16[256,2,4,384]{3,2,1,0:T(4,128)(2,1)}, u32[]{:S(2)}, u32[]{:S(2)}) async-start(bf16[256,2,4,384]{3,2,1,0:T(4,128)(2,1)} %bitcast.185), calls=%async_computation | async-start | bytes 3145728 | tf_op jit(solution)/shard_map/all_to_all | solution.py:71
  67.0 3.1 %copy-start.6 = (bf16[4,256,256]{2,1,0:T(8,128)(2,1)S(1)}, bf16[4,256,256]{2,1,0:T(8,128)(2,1)}, u32[]{:S(2)}) copy-start(bf16[4,256,256]{2,1,0:T(8,128)(2,1)} %param.13) | copy-start | bytes 1572868
  70.8 1.0 copy-start.11
  78.5 7.7 %copy-start.4 = (bf16[256,2,512]{2,0,1:T(8,128)(2,1)S(1)}, bf16[256,2,512]{2,0,1:T(8,128)(2,1)}, u32[]{:S(2)}) copy-start(bf16[256,2,512]{2,0,1:T(8,128)(2,1)} %get-tuple-element.56) | copy-start | bytes 1572868
  78.5 46.1 %all-to-all-start.1 = ((bf16[4,2,256,384]{3,1,0,2:T(2,128)(2,1)}), bf16[4,2,256,384]{3,1,0,2:T(2,128)(2,1)}, u32[]{:S(2)}, u32[]{:S(2)}) async-start(bf16[4,2,256,384]{3,1,0,2:T(2,128)(2,1)} %copy.102), calls=%async_computation.1 | async-start | bytes 3145728 | tf_op jit(solution)/shard_map/all_to_all | solution.py:94
  131.7 2.5 %copy-start.2 = (bf16[512,4,384]{0,2,1:T(8,128)(2,1)S(1)}, bf16[512,4,384]{0,2,1:T(8,128)(2,1)}, u32[]{:S(2)}) copy-start(bf16[512,4,384]{0,2,1:T(8,128)(2,1)} %copy.106) | copy-start | bytes 4718596
  135.4 1.7 copy-start.1
  135.4 1.6 copy-start.9
  137.5 1.6 copy-start.10
  155.0 26.4 %all-to-all-start.2 = ((bf16[1,4,512,384]{3,1,0,2:T(4,128)(2,1)}), bf16[1,4,512,384]{3,1,0,2:T(4,128)(2,1)}, u32[]{:S(2)}, u32[]{:S(2)}) async-start(bf16[1,4,512,384]{3,1,0,2:T(4,128)(2,1)} %copy.111), calls=%async_computation.2 | async-start | bytes 3145728 | tf_op jit(solution)/shard_map/all_to_all | solution.py:119
  181.4 1.9 copy-start.3
  189.9 25.7 %all-to-all-start.3 = ((bf16[4,4,128,384]{3,2,1,0:T(8,128)(2,1)}), bf16[4,4,128,384]{3,2,1,0:T(8,128)(2,1)}, u32[]{:S(2)}, u32[]{:S(2)}) async-start(bf16[4,4,128,384]{3,2,1,0:T(8,128)(2,1)} %pad_maximum_fusion), calls=%async_computation.3 | async-start | bytes 3145728 | tf_op jit(solution)/shard_map/all_to_all | solution.py:131
where the time goes:
time: 219 us; the launch traced here: 218 us
  waiting for transfers between devices  112 us (51%)
  local copies, waits for them, and re-layouts  43 us (20%)
  starting transfers between devices  28.9 us (13%)
  other arithmetic  17.7 us (8%)
  matrix products  15.2 us (7%)
    all_to_all x1, waiting for transfers between devices, local(): lax.all_to_all(analysis, 'lat', split_axis=0, concat_axis=2, tiled=True)  36.7 us
    all_to_all x1, waiting for transfers between devices, local(): lax.all_to_all(synthesis, 'lat', split_axis=2, concat_axis=0, tiled=True)  34 us
    all_to_all x1, waiting for transfers between devices, local(): lax.all_to_all(predicted_field, 'member', split_axis=2, concat_axis=0, ti...  21.8 us
    all_to_all x1, waiting for transfers between devices, local(): lax.all_to_all(grads, 'member', split_axis=0, concat_axis=2, tiled=True)  19.8 us
    all_to_all x1, starting transfers between devices, local(): lax.all_to_all(analysis, 'lat', split_axis=0, concat_axis=2, tiled=True)  12.3 us
    all_to_all x1, starting transfers between devices, local(): lax.all_to_all(synthesis, 'lat', split_axis=2, concat_axis=0, tiled=True)  7.68 us
    dot_general x1, matrix products, local(): jnp.dot(hidden, weight_out, preferred_element_type=jnp.float32)  6.81 us
    unnamed x28, local copies, waits for them, and re-layouts  5.48 us
  transfers between devices with their start and end apart: 4, of which 4 were waited for; matrix products, arithmetic and copies ran while one was open for 3% of the time, Pallas kernels for 0%

commit v1 on v0

v1 whole, which is shorter than its diff:
```python
import functools
import math

import jax
import jax.numpy as jnp
import numpy as np
from jax import lax
from jax.experimental import pallas as pl
from jax.experimental.pallas import tpu as pltpu
from jax.sharding import PartitionSpec as P

EPS_NORM = 1e-05
EPS_DIST = 1e-06
MESH = pl.DeviceIdType.MESH
F32 = jnp.float32
BF16 = jnp.bfloat16


def tables(waves, length):
    m = np.arange(waves)[:, None]
    j = np.arange(length)[None, :]
    angle = (m * j % length) * (2.0 * math.pi / length)
    cosine, sine = np.cos(angle), np.sin(angle)
    forward = np.stack([cosine / length, -sine / length], 1).reshape(2 * waves, length)
    weight = np.where(m == 0, 1.0, 2.0)
    inverse = np.stack([weight * cosine, -weight * sine], 1).reshape(2 * waves, length).T
    return jnp.asarray(forward, BF16), jnp.asarray(inverse, BF16)


def group_order(points, parts):
    rows = np.arange(points * parts)
    part, point = rows // points, rows % points
    order = np.zeros((points * parts, points * parts), np.float32)
    order[rows, point * parts + part] = 1.0
    return jnp.asarray(order, BF16)


def layer_norm(values, scales):
    average = jnp.mean(values, -1, keepdims=True)
    centred = values - average
    spread = jnp.mean(centred * centred, -1, keepdims=True)
    return centred * lax.rsqrt(spread + EPS_NORM) * scales


def inverse_distance(difference):
    return lax.rsqrt(jnp.mean(jnp.square(difference), -1, keepdims=True) + EPS_DIST)


def dot(a, b):
    return jnp.dot(a, b, preferred_element_type=F32)


def kernel(
    x_hbm, obs_hbm, slot_ref, legf_hbm, legi_hbm, filt_hbm, gain1, gain2, win_hbm, wout_hbm,
    cf_hbm, ci_hbm, order_hbm,
    pred_hbm, slope_hbm,
    x, obs, legf, legi, filt, win, wout, cf, ci, order,
    fwd, inv, normed, out_a, in_r, spec, out_b, in_q, pred, in_y, grad, in_z,
    load_sem, x_sem, fs_sem, fr_sem, bs_sem, br_sem, ys_sem, yr_sem, zs_sem, zr_sem, po_sem, so_sem,
):
    members = lax.axis_size("member")
    devices = lax.axis_size("lat")
    me = lax.axis_index("lat")
    mine = lax.axis_index("member")
    rows, length, channels = x.shape
    degrees = legf.shape[1]
    parts = out_a.shape[2]
    slots = parts // 2
    block = length // members
    half = rows // 2
    stride = 27

    def lat_peer(step):
        return (me + stride * step) % devices

    barrier = pltpu.get_barrier_semaphore()

    def greet(step, carry):
        pl.semaphore_signal(barrier, inc=1, device_id=(mine, lat_peer(step)), device_id_type=MESH)
        return carry

    lax.fori_loop(1, devices, greet, 0)
    for step in range(1, members):
        pl.semaphore_signal(
            barrier, inc=1, device_id=((mine + step) % members, me), device_id_type=MESH
        )

    x_loads = [
        pltpu.make_async_copy(x_hbm.at[0, row], x.at[row], x_sem.at[row]) for row in range(rows)
    ]
    sources = [cf_hbm, ci_hbm, order_hbm, legf_hbm, legi_hbm, filt_hbm, win_hbm, wout_hbm]
    places = [cf, ci, order, legf, legi, filt, win, wout]
    loads = [
        pltpu.make_async_copy(source, place, load_sem.at[index])
        for index, (source, place) in enumerate(zip(sources, places))
    ]
    obs_load = pltpu.make_async_copy(
        obs_hbm.at[:, pl.ds(pl.multiple_of(mine * block, block), block), :],
        obs,
        load_sem.at[len(loads)],
    )
    loads[0].start()
    for load in x_loads:
        load.start()
    for load in loads[1:]:
        load.start()
    obs_load.start()

    picks = lax.broadcasted_iota(jnp.int32, (2 * degrees, 2 * degrees), 1)
    picked = jnp.where(slot_ref[...] == picks, 1.0, 0.0).astype(BF16)
    loads[0].wait()
    fwd[...] = dot(picked, cf[...]).astype(BF16)

    def analyse(row):
        def norm_rows(tile, carry):
            at = pl.ds(pl.multiple_of(tile * 128, 128), min(128, length))
            normed[at, :] = layer_norm(x[row, at, :].astype(F32), gain1[...]).astype(BF16)
            return carry

        lax.fori_loop(0, max(length // 128, 1), norm_rows, 0)
        found = dot(fwd[...], normed[...]).astype(BF16)
        out_a[:, row] = found.reshape(devices, parts, channels)

    def send_forward(part):
        def send(step, carry):
            peer = lat_peer(step)
            pltpu.make_async_remote_copy(
                src_ref=out_a.at[peer, pl.ds(part * half, half)],
                dst_ref=in_r.at[me, pl.ds(part * half, half)],
                send_sem=fs_sem.at[part],
                recv_sem=fr_sem.at[part],
                device_id=(mine, peer),
                device_id_type=MESH,
            ).start()
            return carry

        lax.fori_loop(1, devices, send, 0)

    for part in range(2):
        for row in range(part * half, part * half + half):
            x_loads[row].wait()
            analyse(row)
        if part == 0:
            pl.semaphore_wait(barrier, devices - 1 + members - 1)
        send_forward(part)
    in_r[me] = out_a[me]

    loads[1].wait()
    inv[...] = lax.dot_general(
        ci[...], picked, (((1,), (1,)), ((), ())), preferred_element_type=F32
    ).astype(BF16)
    for load in loads[2:]:
        load.wait()
    for slot in range(slots):
        local = slot_ref[pl.ds(pl.multiple_of(me * parts, parts), parts), :][2 * slot : 2 * slot + 1, :]
        level = lax.broadcasted_iota(jnp.int32, (degrees, degrees), 0) * 2
        kept = legf[slot].astype(F32)
        legf[slot] = jnp.where(level >= local, kept, 0.0).astype(BF16)

    for part in range(2):
        everything = in_r.at[pl.ds(0, devices - 1), pl.ds(0, half)]
        pltpu.make_async_copy(everything, everything, fr_sem.at[part]).wait()

    group = order.shape[0] // (rows * parts)
    points = group * rows

    def gather(index, carry):
        taken = in_r[pl.ds(index * group, group)].reshape(points * parts, channels)
        moved = dot(order[...], taken).astype(BF16)
        at = pl.ds(pl.multiple_of(index * points, points), points)
        spec[:, at, :] = moved.reshape(parts, points, channels)
        return carry

    lax.fori_loop(0, devices // group, gather, 0)

    def transform(slot, carry):
        real = dot(legf[slot], spec[2 * slot])
        imag = dot(legf[slot], spec[2 * slot + 1])
        new_real = (real * filt[0] - imag * filt[1]).astype(BF16)
        new_imag = (real * filt[1] + imag * filt[0]).astype(BF16)
        spec[2 * slot] = dot(legi[slot], new_real).astype(BF16)
        spec[2 * slot + 1] = dot(legi[slot], new_imag).astype(BF16)
        return carry

    lax.fori_loop(0, slots, transform, 0)

    def scatter(index, carry):
        at = pl.ds(pl.multiple_of(index * points, points), points)
        taken = spec[:, at, :].reshape(points * parts, channels)
        moved = lax.dot_general(
            order[...], taken, (((0,), (0,)), ((), ())), preferred_element_type=F32
        ).astype(BF16)
        out_b[pl.ds(index * group, group)] = moved.reshape(group, rows, parts, channels)
        return carry

    lax.fori_loop(0, devices // group, scatter, 0)

    def send_back(row, carry):
        def send(step, inner):
            peer = lat_peer(step)
            pltpu.make_async_remote_copy(
                src_ref=out_b.at[peer, row],
                dst_ref=in_q.at[row, me],
                send_sem=bs_sem.at[row],
                recv_sem=br_sem.at[row],
                device_id=(mine, peer),
                device_id_type=MESH,
            ).start()
            return inner

        lax.fori_loop(1, devices, send, 0)
        in_q[row, me] = out_b[me, row]
        return carry

    lax.fori_loop(0, rows, send_back, 0)
    obs_load.wait()

    tall = min(256, length)

    def member_copies(row, source, place, send_sem, recv_sem):
        copies = []
        for step in range(1, members):
            peer = (mine + step) % members
            copies.append(
                pltpu.make_async_remote_copy(
                    src_ref=source(row, peer),
                    dst_ref=place.at[row, mine],
                    send_sem=send_sem.at[row],
                    recv_sem=recv_sem.at[row],
                    device_id=(peer, me),
                    device_id_type=MESH,
                )
            )
        return copies

    def predict(row):
        arrived = in_q.at[row, pl.ds(0, devices - 1)]
        pltpu.make_async_copy(arrived, arrived, br_sem.at[row]).wait()

        def predict_rows(tile, carry):
            at = pl.ds(pl.multiple_of(tile * tall, tall), tall)
            waves = in_q[row].reshape(devices * parts, channels)
            after = x[row, at, :].astype(F32) + dot(inv[at, :], waves)
            second = layer_norm(after, gain2[...]).astype(BF16)
            hidden = jax.nn.gelu(dot(second, win[...])).astype(BF16)
            pred[row, at, :] = (after + dot(hidden, wout[...])).astype(BF16)
            return carry

        lax.fori_loop(0, length // tall, predict_rows, 0)
        at_peer = lambda index, peer: pred.at[
            index, pl.ds(pl.multiple_of(peer * block, block), block), :
        ]
        for copy in member_copies(row, at_peer, in_y, ys_sem, yr_sem):
            copy.start()
        pltpu.make_async_copy(pred.at[row], pred_hbm.at[0, row], po_sem.at[row]).start()

    thin = min(32, block)

    def score(row):
        arrived = in_y.at[row, pl.ds(0, members - 1)]
        pltpu.make_async_copy(arrived, arrived, yr_sem.at[row]).wait()
        in_y[row, mine] = pred[row, pl.ds(pl.multiple_of(mine * block, block), block), :]

        def score_rows(tile, carry):
            at = pl.ds(pl.multiple_of(tile * thin, thin), thin)
            fields = [in_y[row, index, at, :].astype(F32) for index in range(members)]
            target = obs[row, at, :].astype(F32)
            slopes = []
            for index in range(members):
                gap = fields[index] - target
                slopes.append(gap * inverse_distance(gap))
            for first in range(members):
                for second in range(first + 1, members):
                    gap = fields[first] - fields[second]
                    pull = gap * (inverse_distance(gap) * (1.0 / (members - 1)))
                    slopes[first] = slopes[first] - pull
                    slopes[second] = slopes[second] + pull
            for index in range(members):
                grad[row, index, at, :] = slopes[index].astype(BF16)
            return carry

        lax.fori_loop(0, block // thin, score_rows, 0)
        for copy in member_copies(row, lambda index, peer: grad.at[index, peer], in_z, zs_sem, zr_sem):
            copy.start()
        in_z[row, mine] = grad[row, mine]

    def finish(row, carry):
        predict(row)

        @pl.when(row > 0)
        def _():
            score(row - 1)

        return carry

    lax.fori_loop(0, rows, finish, 0)
    score(rows - 1)

    def deliver(row, carry):
        arrived = in_z.at[row, pl.ds(0, members - 1)]
        pltpu.make_async_copy(arrived, arrived, zr_sem.at[row]).wait()
        pltpu.make_async_copy(in_z.at[row], slope_hbm.at[0, row], so_sem.at[row]).start()
        return carry

    lax.fori_loop(0, rows, deliver, 0)

    for part in range(2):
        sent = out_a.at[pl.ds(0, devices - 1), pl.ds(0, half)]
        pltpu.make_async_copy(sent, sent, fs_sem.at[part]).wait()

    def drain(row, carry):
        sent = in_q.at[row, pl.ds(0, devices - 1)]
        pltpu.make_async_copy(sent, sent, bs_sem.at[row]).wait()
        sent = in_y.at[row, pl.ds(0, members - 1)]
        pltpu.make_async_copy(sent, sent, ys_sem.at[row]).wait()
        pltpu.make_async_copy(sent, sent, zs_sem.at[row]).wait()
        pltpu.make_async_copy(pred.at[row], pred_hbm.at[0, row], po_sem.at[row]).wait()
        pltpu.make_async_copy(in_z.at[row], slope_hbm.at[0, row], so_sem.at[row]).wait()
        return carry

    lax.fori_loop(0, rows, drain, 0)


def local(
    ensemble_starting_fields, observed, wave_of_slot, leg_forward, leg_inverse, spec_filter,
    gain_first, gain_second, weight_in, weight_out,
):
    _, rows, length, channels = ensemble_starting_fields.shape
    waves = wave_of_slot.shape[0]
    slots, degrees, lats = leg_forward.shape
    hidden = weight_in.shape[1]
    devices = lax.axis_size("lat")
    members = lax.axis_size("member")
    block = length // members
    parts = 2 * slots
    forward, inverse = tables(waves, length)
    group = min(8, devices)
    order = group_order(group * rows, parts)
    picks = (2 * wave_of_slot[:, None] + jnp.arange(2, dtype=jnp.int32)[None, :]).reshape(-1, 1)
    whole = pl.BlockSpec(memory_space=pl.ANY)
    near = pl.BlockSpec(memory_space=pltpu.VMEM)
    shape = jax.ShapeDtypeStruct((1, rows, length, channels), BF16)
    sems = pltpu.SemaphoreType.DMA
    pred, slope = pl.pallas_call(
        kernel,
        out_shape=(shape, jax.ShapeDtypeStruct((1, rows, members, block, channels), BF16)),
        in_specs=[whole, whole, near, whole, whole, whole, near, near] + [whole] * 5,
        out_specs=(whole, whole),
        scratch_shapes=[
            pltpu.VMEM((rows, length, channels), BF16),
            pltpu.VMEM((rows, block, channels), BF16),
            pltpu.VMEM((slots, degrees, lats), BF16),
            pltpu.VMEM((slots, lats, degrees), BF16),
            pltpu.VMEM((2, degrees, channels), F32),
            pltpu.VMEM((channels, hidden), BF16),
            pltpu.VMEM((hidden, channels), BF16),
            pltpu.VMEM((2 * waves, length), BF16),
            pltpu.VMEM((length, 2 * waves), BF16),
            pltpu.VMEM(order.shape, BF16),
            pltpu.VMEM((2 * waves, length), BF16),
            pltpu.VMEM((length, 2 * waves), BF16),
            pltpu.VMEM((length, channels), BF16),
            pltpu.VMEM((devices, rows, parts, channels), BF16),
            pltpu.VMEM((devices, rows, parts, channels), BF16),
            pltpu.VMEM((parts, lats, channels), BF16),
            pltpu.VMEM((devices, rows, parts, channels), BF16),
            pltpu.VMEM((rows, devices, parts, channels), BF16),
            pltpu.VMEM((rows, length, channels), BF16),
            pltpu.VMEM((rows, members, block, channels), BF16),
            pltpu.VMEM((rows, members, block, channels), BF16),
            pltpu.VMEM((rows, members, block, channels), BF16),
            sems((9,)),
            sems((rows,)),
            sems((2,)),
            sems((2,)),
            sems((rows,)),
            sems((rows,)),
            sems((rows,)),
            sems((rows,)),
            sems((rows,)),
            sems((rows,)),
            sems((rows,)),
            sems((rows,)),
        ],
        compiler_params=pltpu.CompilerParams(
            collective_id=0, has_side_effects=True, vmem_limit_bytes=60 * 1024 * 1024
        ),
    )(
        ensemble_starting_fields, observed, picks, leg_forward, leg_inverse, spec_filter,
        gain_first[None, :], gain_second[None, :], weight_in, weight_out, forward, inverse, order,
    )
    return (pred, slope.reshape(pred.shape))


def solution(mesh):
    in_specs = (
        P("member", "lat", None, None),
        P("lat", None, None),
        P(),
        P("lat", None, None),
        P("lat", None, None),
        P(),
        P(),
        P(),
        P(),
        P(),
    )
    out_specs = (P("member", "lat", None, None), P("member", "lat", None, None))
    return jax.shard_map(local, mesh=mesh, in_specs=in_specs, out_specs=out_specs, check_vma=False)
```

time: 219 us -> 121 us (0.55)
  Pallas kernels: 0 us -> 112 us
  waiting for transfers between devices: 112 us -> 0 us
  local copies, waits for them, and re-layouts: 43 us -> 7.3 us
  starting transfers between devices: 28.9 us -> 0 us
  other arithmetic: 17.7 us -> 0.78 us
  matrix products: 15.2 us -> 0 us
    all_to_all x4 -> x0, waiting for transfers between devices: 112 us -> none  [the longest x1 36.7 us: local(): lax.all_to_all(analysis, 'lat', split_axis=0, concat_axis=2, tiled=True)]
    pallas_call x0 -> x1, Pallas kernels: none -> 112 us  [local(): pl.pallas_call(kernel, out_shape=(shape, jax.ShapeDtypeStruct((1, rows, m...]
    all_to_all x4 -> x0, starting transfers between devices: 28.9 us -> none  [the longest x1 12.3 us: local(): lax.all_to_all(analysis, 'lat', split_axis=0, concat_axis=2, tiled=True)]
    dot_general x7 -> x0, matrix products: 15.2 us -> none  [the longest x1 6.81 us: local(): jnp.dot(hidden, weight_out, preferred_element_type=jnp.float32)]
    convert_element_type x10 -> x0, local copies, waits for them, and re-layouts: 13.1 us -> none  [the longest x4 5.14 us: split_table(): table_low = (table - table_high.astype(jnp.float32)).astype(jnp.bfloat16)]
    all_to_all x4 -> x0, local copies, waits for them, and re-layouts: 11 us -> none  [the longest x1 3.36 us: local(): lax.all_to_all(synthesis, 'lat', split_axis=2, concat_axis=0, tiled=True)]
    reshape x3 -> x0, local copies, waits for them, and re-layouts: 9.67 us -> none  [the longest x1 3.73 us: local(): returned = returned.reshape(2 * waves_all, lat_rows, channels)]
    another operation x6 -> x0, other arithmetic: 4.54 us -> none  [the longest x5 4.04 us: local(): grads = jnp.stack(grads, 0).astype(jnp.bfloat16)]
  transfers between devices with their start and end apart: 4 -> 0, of which waited for: 4 -> 0; matrix products, arithmetic and copies ran while one was open for 3% -> 0% of each run, Pallas kernels for 0% -> 0%
where the time goes in v1:
time: 121 us
  Pallas kernels  112 us (93%)
  local copies, waits for them, and re-layouts  7.3 us (6%)
    pallas_call x1, Pallas kernels, local(): pl.pallas_call(kernel, out_shape=(shape, jax.ShapeDtypeStruct((1, rows, m...  112 us
    unnamed x4, local copies, waits for them, and re-layouts  3.97 us

profile of v1, /device:TPU:2, one launch (start us, length us, event | category | flops | bytes accessed | tf_op | source)
XLA Modules:
  0.0 120.6 jit_solution(13603879137858338739)
XLA Ops:
  0.6 0.7 broadcast_multiply_fusion
  1.3 1.2 %broadcast_in_dim.8.gain1 = f32[1,384]{1,0:T(1,128)} reshape(f32[384]{0:T(512)} %param.19) | data formatting | bytes 3072 | tf_op jit(solution)/shard_map/broadcast_in_dim | solution.py:390
  2.6 1.3 %broadcast_in_dim.9.gain2 = f32[1,384]{1,0:T(1,128)} reshape(f32[384]{0:T(512)} %param.20) | data formatting | bytes 3072 | tf_op jit(solution)/shard_map/broadcast_in_dim | solution.py:390
  3.8 0.1 iota_add_fusion
  3.9 0.8 add.27.slot_ref
  4.7 111.9 %shard_map.140 = (bf16[1,4,512,384]{3,2,1,0:T(8,128)(2,1)}, bf16[1,4,4,128,384]{4,3,2,1,0:T(8,128)(2,1)}) custom-call(bf16[1,4,512,384]{3,2,1,0:T(8,128)(2,1)} %x_hbm.1, bf16[4,512,384]{2,1,0:T(8,128)(2,1)} %obs_hbm.1, s32[512,1]{1,0:T(8,128)} %add.27.slot_ref, bf16[4,256,256]{2,1,0:T(8,128)(2,1)} %legf_hbm.1, bf16[4,256,256]{2,1,0:T(8,128)(2,1)} %legi_hbm.1, ...), custom_call_target="tpu_custom_call" | custom-call | tf_op jit(solution)/shard_map/pallas_call | solution.py:344
  116.6 0.0 copy-start
  116.6 2.8 %copy.18 = bf16[1,4,512,384]{3,2,1,0:T(8,128)(2,1)} copy(bf16[1,4,512,384]{3,2,1,0:T(8,128)(2,1)} %get-tuple-element.8) | data formatting | bytes 3145728
  119.5 0.0 copy-done
  119.5 1.1 copy.19
Async XLA Ops:
  116.6 2.8 %copy-start = (bf16[1,4,4,128,384]{4,3,2,1,0:T(8,128)(2,1)S(1)}, bf16[1,4,4,128,384]{4,3,2,1,0:T(8,128)(2,1)}, u32[]{:S(2)}) copy-start(bf16[1,4,4,128,384]{4,3,2,1,0:T(8,128)(2,1)} %get-tuple-element.5) | copy-start | bytes 4718596

commit v2 on v1

--- a/solution.py
+++ b/solution.py
@@ -51,12 +51,13 @@
 
 
 def kernel(
-    x_hbm, obs_hbm, slot_ref, legf_hbm, legi_hbm, filt_hbm, gain1, gain2, win_hbm, wout_hbm,
+    x_hbm, obs_hbm, slot_hbm, legf_hbm, legi_hbm, filt_hbm, gain1_hbm, gain2_hbm, win_hbm, wout_hbm,
     cf_hbm, ci_hbm, order_hbm,
-    pred_hbm, slope_hbm,
+    pred, in_z,
     x, obs, legf, legi, filt, win, wout, cf, ci, order,
-    fwd, inv, normed, out_a, in_r, spec, out_b, in_q, pred, in_y, grad, in_z,
-    load_sem, x_sem, fs_sem, fr_sem, bs_sem, br_sem, ys_sem, yr_sem, zs_sem, zr_sem, po_sem, so_sem,
+    fwd, inv, normed, out_a, in_r, spec, out_b, in_q, in_y, grad,
+    slot_ref, slot_smem, gain1, gain2,
+    load_sem, x_sem, fs_sem, fr_sem, bs_sem, br_sem, ys_sem, yr_sem, zs_sem, zr_sem, small_sem,
 ):
     members = lax.axis_size("member")
     devices = lax.axis_size("lat")
@@ -68,7 +69,7 @@
     slots = parts // 2
     block = length // members
     half = rows // 2
-    stride = 27
+    stride = 1
 
     def lat_peer(step):
         return (me + stride * step) % devices
@@ -99,6 +100,14 @@
         obs,
         load_sem.at[len(loads)],
     )
+    small = [
+        pltpu.make_async_copy(source, place, small_sem.at[index])
+        for index, (source, place) in enumerate(
+            [(slot_hbm, slot_ref), (gain1_hbm, gain1), (gain2_hbm, gain2), (slot_hbm, slot_smem)]
+        )
+    ]
+    for load in small:
+        load.start()
     loads[0].start()
     for load in x_loads:
         load.start()
@@ -106,15 +115,25 @@
         load.start()
     obs_load.start()
 
-    picks = lax.broadcasted_iota(jnp.int32, (2 * degrees, 2 * degrees), 1)
-    picked = jnp.where(slot_ref[...] == picks, 1.0, 0.0).astype(BF16)
+    for load in small:
+        load.wait()
+    spread = (degrees, 2 * degrees)
+    gap = lax.broadcasted_iota(jnp.int32, spread, 1) - 2 * lax.broadcasted_iota(jnp.int32, spread, 0)
+    twice = jnp.where((gap == 0) | (gap == 1), 2.0, 0.0).astype(BF16)
+    waves = jnp.broadcast_to(slot_ref[...].astype(F32)[None, :], (8, degrees)).astype(BF16)
+    columns = dot(waves, twice)[0:1].astype(jnp.int32)
+    square = (2 * degrees, 2 * degrees)
+    columns = columns + lax.broadcasted_iota(jnp.int32, (1, 2 * degrees), 1) % 2
+    picked = jnp.where(lax.broadcasted_iota(jnp.int32, square, 0) == columns, 1.0, 0.0).astype(BF16)
     loads[0].wait()
-    fwd[...] = dot(picked, cf[...]).astype(BF16)
+    fwd[...] = lax.dot_general(
+        picked, cf[...], (((0,), (0,)), ((), ())), preferred_element_type=F32
+    ).astype(BF16)
 
     def analyse(row):
         def norm_rows(tile, carry):
             at = pl.ds(pl.multiple_of(tile * 128, 128), min(128, length))
-            normed[at, :] = layer_norm(x[row, at, :].astype(F32), gain1[...]).astype(BF16)
+            normed[at, :] = layer_norm(x[row, at, :].astype(F32), gain1[...][None, :]).astype(BF16)
             return carry
 
         lax.fori_loop(0, max(length // 128, 1), norm_rows, 0)
@@ -146,14 +165,12 @@
     in_r[me] = out_a[me]
 
     loads[1].wait()
-    inv[...] = lax.dot_general(
-        ci[...], picked, (((1,), (1,)), ((), ())), preferred_element_type=F32
-    ).astype(BF16)
+    inv[...] = dot(ci[...], picked).astype(BF16)
     for load in loads[2:]:
         load.wait()
     for slot in range(slots):
-        local = slot_ref[pl.ds(pl.multiple_of(me * parts, parts), parts), :][2 * slot : 2 * slot + 1, :]
-        level = lax.broadcasted_iota(jnp.int32, (degrees, degrees), 0) * 2
+        local = slot_smem[me * slots + slot]
+        level = lax.broadcasted_iota(jnp.int32, (degrees, degrees), 0)
         kept = legf[slot].astype(F32)
         legf[slot] = jnp.where(level >= local, kept, 0.0).astype(BF16)
 
@@ -241,7 +258,7 @@
             at = pl.ds(pl.multiple_of(tile * tall, tall), tall)
             waves = in_q[row].reshape(devices * parts, channels)
             after = x[row, at, :].astype(F32) + dot(inv[at, :], waves)
-            second = layer_norm(after, gain2[...]).astype(BF16)
+            second = layer_norm(after, gain2[...][None, :]).astype(BF16)
             hidden = jax.nn.gelu(dot(second, win[...])).astype(BF16)
             pred[row, at, :] = (after + dot(hidden, wout[...])).astype(BF16)
             return carry
@@ -252,7 +269,6 @@
         ]
         for copy in member_copies(row, at_peer, in_y, ys_sem, yr_sem):
             copy.start()
-        pltpu.make_async_copy(pred.at[row], pred_hbm.at[0, row], po_sem.at[row]).start()
 
     thin = min(32, block)
 
@@ -299,7 +315,6 @@
     def deliver(row, carry):
         arrived = in_z.at[row, pl.ds(0, members - 1)]
         pltpu.make_async_copy(arrived, arrived, zr_sem.at[row]).wait()
-        pltpu.make_async_copy(in_z.at[row], slope_hbm.at[0, row], so_sem.at[row]).start()
         return carry
 
     lax.fori_loop(0, rows, deliver, 0)
@@ -314,11 +329,20 @@
         sent = in_y.at[row, pl.ds(0, members - 1)]
         pltpu.make_async_copy(sent, sent, ys_sem.at[row]).wait()
         pltpu.make_async_copy(sent, sent, zs_sem.at[row]).wait()
-        pltpu.make_async_copy(pred.at[row], pred_hbm.at[0, row], po_sem.at[row]).wait()
-        pltpu.make_async_copy(in_z.at[row], slope_hbm.at[0, row], so_sem.at[row]).wait()
         return carry
 
     lax.fori_loop(0, rows, drain, 0)
+
+
+def store(pred, slope, pred_out, slope_out, sem):
+    copies = [
+        pltpu.make_async_copy(pred, pred_out.at[0], sem.at[0]),
+        pltpu.make_async_copy(slope, slope_out.at[0], sem.at[1]),
+    ]
+    for copy in copies:
+        copy.start()
+    for copy in copies:
+        copy.wait()
 
 
 def local(
@@ -336,16 +360,22 @@
     forward, inverse = tables(waves, length)
     group = min(8, devices)
     order = group_order(group * rows, parts)
-    picks = (2 * wave_of_slot[:, None] + jnp.arange(2, dtype=jnp.int32)[None, :]).reshape(-1, 1)
-    whole = pl.BlockSpec(memory_space=pl.ANY)
+    whole = pl.BlockSpec(memory_space=pltpu.HBM)
     near = pl.BlockSpec(memory_space=pltpu.VMEM)
-    shape = jax.ShapeDtypeStruct((1, rows, length, channels), BF16)
     sems = pltpu.SemaphoreType.DMA
+    operands = [
+        ensemble_starting_fields, observed, wave_of_slot, leg_forward, leg_inverse, spec_filter,
+        gain_first, gain_second, weight_in, weight_out, forward, inverse, order,
+    ]
+    operands = [pltpu.with_memory_space_constraint(operand, pltpu.HBM) for operand in operands]
     pred, slope = pl.pallas_call(
         kernel,
-        out_shape=(shape, jax.ShapeDtypeStruct((1, rows, members, block, channels), BF16)),
-        in_specs=[whole, whole, near, whole, whole, whole, near, near] + [whole] * 5,
-        out_specs=(whole, whole),
+        out_shape=(
+            pltpu.VMEM((rows, length, channels), BF16),
+            pltpu.VMEM((rows, members, block, channels), BF16),
+        ),
+        in_specs=[whole] * 13,
+        out_specs=(near, near),
         scratch_shapes=[
             pltpu.VMEM((rows, length, channels), BF16),
             pltpu.VMEM((rows, block, channels), BF16),
@@ -365,10 +395,12 @@
             pltpu.VMEM((parts, lats, channels), BF16),
             pltpu.VMEM((devices, rows, parts, channels), BF16),
             pltpu.VMEM((rows, devices, parts, channels), BF16),
-            pltpu.VMEM((rows, length, channels), BF16),
             pltpu.VMEM((rows, members, block, channels), BF16),
             pltpu.VMEM((rows, members, block, channels), BF16),
-            pltpu.VMEM((rows, members, block, channels), BF16),
+            pltpu.VMEM((waves,), jnp.int32),
+            pltpu.SMEM((waves,), jnp.int32),
+            pltpu.VMEM((channels,), F32),
+            pltpu.VMEM((channels,), F32),
             sems((9,)),
             sems((rows,)),
             sems((2,)),
@@ -379,17 +411,23 @@
             sems((rows,)),
             sems((rows,)),
             sems((rows,)),
-            sems((rows,)),
-            sems((rows,)),
+            sems((4,)),
         ],
         compiler_params=pltpu.CompilerParams(
-            collective_id=0, has_side_effects=True, vmem_limit_bytes=60 * 1024 * 1024
+            collective_id=0, has_side_effects=True, vmem_limit_bytes=48 * 1024 * 1024
         ),
-    )(
-        ensemble_starting_fields, observed, picks, leg_forward, leg_inverse, spec_filter,
-        gain_first[None, :], gain_second[None, :], weight_in, weight_out, forward, inverse, order,
-    )
-    return (pred, slope.reshape(pred.shape))
+    )(*operands)
+    results = [pred, slope.reshape(rows, length, channels)]
+    results = [pltpu.with_memory_space_constraint(result, pltpu.VMEM) for result in results]
+    shape = jax.ShapeDtypeStruct((1, rows, length, channels), BF16)
+    pred, slope = pl.pallas_call(
+        store,
+        out_shape=(shape, shape),
+        in_specs=[near, near],
+        out_specs=(whole, whole),
+        scratch_shapes=[sems((2,))],
+    )(*results)
+    return (pred, slope)
 
 
 def solution(mesh):

time: 121 us -> 114 us (0.942); the launches traced: 121 us -> 112 us
  local copies, waits for them, and re-layouts: 7.3 us -> 0 us
    unnamed x4 -> x0, local copies, waits for them, and re-layouts: 3.97 us -> none
    broadcast_in_dim x2 -> x0, local copies, waits for them, and re-layouts: 2.52 us -> none  [the longest x1 1.27 us: local(): gain_second[None, :]]
    pallas_call x1 -> x2, Pallas kernels: 112 us -> 112 us  [the longest x1 110 us: local(): pl.pallas_call(kernel, out_shape=(pltpu.VMEM((rows, length, channels), BF...]
where the time goes in v2:
time: 114 us; the launch traced here: 112 us
  Pallas kernels  112 us (98%)
    pallas_call x1, Pallas kernels, local(): pl.pallas_call(kernel, out_shape=(pltpu.VMEM((rows, length, channels), BF...  110 us

profile of v2, /device:TPU:2, one launch (start us, length us, event | category | flops | bytes accessed | tf_op | source)
XLA Modules:
  0.0 112.4 jit_solution(15211750220818166139)
XLA Ops:
  0.6 110.1 %shard_map.140 = (bf16[4,512,384]{2,1,0:T(8,128)(2,1)S(1)}, bf16[4,4,128,384]{3,2,1,0:T(8,128)(2,1)S(1)}) custom-call(bf16[1,4,512,384]{3,2,1,0:T(8,128)(2,1)} %x_hbm.1, bf16[4,512,384]{2,1,0:T(8,128)(2,1)} %obs_hbm.1, s32[256]{0:T(256)} %slot_hbm.1, bf16[4,256,256]{2,1,0:T(8,128)(2,1)} %legf_hbm.1, bf16[4,256,256]{2,1,0:T(8,128)(2,1)} %legi_hbm.1, ...), custom_call_target="tpu_custom_call" | custom-call | tf_op jit(solution)/shard_map/pallas_call | solution.py:371
  110.7 1.7 %shard_map.141 = (bf16[1,4,512,384]{3,2,1,0:T(8,128)(2,1)}, bf16[1,4,512,384]{3,2,1,0:T(8,128)(2,1)}) custom-call(bf16[4,512,384]{2,1,0:T(8,128)(2,1)S(1)} %get-tuple-element.4.pred, bf16[4,512,384]{2,1,0:T(8,128)(2,1)S(1)} %bitcast.1), custom_call_target="tpu_custom_call" | custom-call | tf_op jit(solution)/shard_map/pallas_call | solution.py:423

commit v3 on v2

--- a/solution.py
+++ b/solution.py
@@ -68,7 +68,6 @@
     parts = out_a.shape[2]
     slots = parts // 2
     block = length // members
-    half = rows // 2
     stride = 1
 
     def lat_peer(step):
@@ -130,22 +129,39 @@
         picked, cf[...], (((0,), (0,)), ((), ())), preferred_element_type=F32
     ).astype(BF16)
 
-    def analyse(row):
-        def norm_rows(tile, carry):
-            at = pl.ds(pl.multiple_of(tile * 128, 128), min(128, length))
-            normed[at, :] = layer_norm(x[row, at, :].astype(F32), gain1[...][None, :]).astype(BF16)
-            return carry
-
-        lax.fori_loop(0, max(length // 128, 1), norm_rows, 0)
-        found = dot(fwd[...], normed[...]).astype(BF16)
-        out_a[:, row] = found.reshape(devices, parts, channels)
-
-    def send_forward(part):
+    first = 2 * channels // 3 // 128 * 128
+    chunks = [(0, first), (first, channels - first)]
+
+    def norm_rows(row, carry):
+        def norm_tile(tile, inner):
+            at = pl.ds(pl.multiple_of(tile * wide, wide), wide)
+            normed[row, at, :] = layer_norm(x[row, at, :].astype(F32), gain1[...][None, :]).astype(BF16)
+            return inner
+
+        return lax.fori_loop(0, length // wide, norm_tile, carry)
+
+    wide = min(128, length)
+    for row in range(rows):
+        x_loads[row].wait()
+        norm_rows(row, 0)
+
+    for part, (lane, width) in enumerate(chunks):
+        lanes = pl.ds(lane, width)
+
+        def analyse(row, carry):
+            found = dot(fwd[...], normed[row, :, lanes]).astype(BF16)
+            out_a[:, row, :, lanes] = found.reshape(devices, parts, width)
+            return carry
+
+        lax.fori_loop(0, rows, analyse, 0)
+        if part == 0:
+            pl.semaphore_wait(barrier, devices - 1 + members - 1)
+
         def send(step, carry):
             peer = lat_peer(step)
             pltpu.make_async_remote_copy(
-                src_ref=out_a.at[peer, pl.ds(part * half, half)],
-                dst_ref=in_r.at[me, pl.ds(part * half, half)],
+                src_ref=out_a.at[peer, :, :, lanes],
+                dst_ref=in_r.at[me, :, :, lanes],
                 send_sem=fs_sem.at[part],
                 recv_sem=fr_sem.at[part],
                 device_id=(mine, peer),
@@ -154,14 +170,6 @@
             return carry
 
         lax.fori_loop(1, devices, send, 0)
-
-    for part in range(2):
-        for row in range(part * half, part * half + half):
-            x_loads[row].wait()
-            analyse(row)
-        if part == 0:
-            pl.semaphore_wait(barrier, devices - 1 + members - 1)
-        send_forward(part)
     in_r[me] = out_a[me]
 
     loads[1].wait()
@@ -174,161 +182,177 @@
         kept = legf[slot].astype(F32)
         legf[slot] = jnp.where(level >= local, kept, 0.0).astype(BF16)
 
-    for part in range(2):
-        everything = in_r.at[pl.ds(0, devices - 1), pl.ds(0, half)]
-        pltpu.make_async_copy(everything, everything, fr_sem.at[part]).wait()
-
     group = order.shape[0] // (rows * parts)
     points = group * rows
 
-    def gather(index, carry):
-        taken = in_r[pl.ds(index * group, group)].reshape(points * parts, channels)
-        moved = dot(order[...], taken).astype(BF16)
-        at = pl.ds(pl.multiple_of(index * points, points), points)
-        spec[:, at, :] = moved.reshape(parts, points, channels)
-        return carry
-
-    lax.fori_loop(0, devices // group, gather, 0)
-
-    def transform(slot, carry):
-        real = dot(legf[slot], spec[2 * slot])
-        imag = dot(legf[slot], spec[2 * slot + 1])
-        new_real = (real * filt[0] - imag * filt[1]).astype(BF16)
-        new_imag = (real * filt[1] + imag * filt[0]).astype(BF16)
-        spec[2 * slot] = dot(legi[slot], new_real).astype(BF16)
-        spec[2 * slot + 1] = dot(legi[slot], new_imag).astype(BF16)
-        return carry
-
-    lax.fori_loop(0, slots, transform, 0)
-
-    def scatter(index, carry):
-        at = pl.ds(pl.multiple_of(index * points, points), points)
-        taken = spec[:, at, :].reshape(points * parts, channels)
-        moved = lax.dot_general(
-            order[...], taken, (((0,), (0,)), ((), ())), preferred_element_type=F32
-        ).astype(BF16)
-        out_b[pl.ds(index * group, group)] = moved.reshape(group, rows, parts, channels)
-        return carry
-
-    lax.fori_loop(0, devices // group, scatter, 0)
-
-    def send_back(row, carry):
-        def send(step, inner):
+    def send_back(row, lanes):
+        def send(step, carry):
             peer = lat_peer(step)
             pltpu.make_async_remote_copy(
-                src_ref=out_b.at[peer, row],
-                dst_ref=in_q.at[row, me],
+                src_ref=out_b.at[peer, row, :, lanes],
+                dst_ref=in_q.at[row, me, :, lanes],
                 send_sem=bs_sem.at[row],
                 recv_sem=br_sem.at[row],
                 device_id=(mine, peer),
                 device_id_type=MESH,
             ).start()
-            return inner
+            return carry
 
         lax.fori_loop(1, devices, send, 0)
+
+    for part, (lane, width) in enumerate(chunks):
+        lanes = pl.ds(lane, width)
+        everything = in_r.at[pl.ds(0, devices - 1), :, :, lanes]
+        pltpu.make_async_copy(everything, everything, fr_sem.at[part]).wait()
+
+        def gather(index, carry):
+            taken = in_r[pl.ds(index * group, group), :, :, lanes].reshape(points * parts, width)
+            moved = dot(order[...], taken).astype(BF16)
+            at = pl.ds(pl.multiple_of(index * points, points), points)
+            spec[:, at, lanes] = moved.reshape(parts, points, width)
+            return carry
+
+        lax.fori_loop(0, devices // group, gather, 0)
+
+        def transform(slot, carry):
+            real = dot(legf[slot], spec[2 * slot, :, lanes])
+            imag = dot(legf[slot], spec[2 * slot + 1, :, lanes])
+            filt_real, filt_imag = filt[0, :, lanes], filt[1, :, lanes]
+            new_real = (real * filt_real - imag * filt_imag).astype(BF16)
+            new_imag = (real * filt_imag + imag * filt_real).astype(BF16)
+            spec[2 * slot, :, lanes] = dot(legi[slot], new_real).astype(BF16)
+            spec[2 * slot + 1, :, lanes] = dot(legi[slot], new_imag).astype(BF16)
+            return carry
+
+        lax.fori_loop(0, slots, transform, 0)
+
+        def scatter(index, carry):
+            at = pl.ds(pl.multiple_of(index * points, points), points)
+            taken = spec[:, at, lanes].reshape(points * parts, width)
+            moved = lax.dot_general(
+                order[...], taken, (((0,), (0,)), ((), ())), preferred_element_type=F32
+            ).astype(BF16)
+            out_b[pl.ds(index * group, group), :, :, lanes] = moved.reshape(group, rows, parts, width)
+            return carry
+
+        lax.fori_loop(0, devices // group, scatter, 0)
+        send_back(0, lanes)
+
+    everywhere = pl.ds(0, channels)
+
+    def send_rest(row, carry):
+        send_back(row, everywhere)
+        return carry
+
+    lax.fori_loop(1, rows, send_rest, 0)
+    for row in range(rows):
         in_q[row, me] = out_b[me, row]
-        return carry
-
-    lax.fori_loop(0, rows, send_back, 0)
     obs_load.wait()
 
-    tall = min(256, length)
-
-    def member_copies(row, source, place, send_sem, recv_sem):
-        copies = []
+    halves = in_y.shape[1]
+    piece = block // halves
+    thin = min(32, piece)
+
+    def spans(half):
+        return [
+            pl.ds(pl.multiple_of(index * block + half * piece, piece), piece)
+            for index in range(members)
+        ]
+
+    def predict(row, half):
+        waves = in_q[row].reshape(devices * parts, channels)
+        table = jnp.concatenate([inv[at, :] for at in spans(half)], 0)
+        before = jnp.concatenate([x[row, at, :] for at in spans(half)], 0)
+        after = before.astype(F32) + dot(table, waves)
+        second = layer_norm(after, gain2[...][None, :]).astype(BF16)
+        hidden = jax.nn.gelu(dot(second, win[...])).astype(BF16)
+        result = (after + dot(hidden, wout[...])).astype(BF16)
+        for index, at in enumerate(spans(half)):
+            pred[row, at, :] = result[index * piece : (index + 1) * piece]
         for step in range(1, members):
             peer = (mine + step) % members
-            copies.append(
-                pltpu.make_async_remote_copy(
-                    src_ref=source(row, peer),
-                    dst_ref=place.at[row, mine],
-                    send_sem=send_sem.at[row],
-                    recv_sem=recv_sem.at[row],
-                    device_id=(peer, me),
-                    device_id_type=MESH,
-                )
-            )
-        return copies
-
-    def predict(row):
-        arrived = in_q.at[row, pl.ds(0, devices - 1)]
-        pltpu.make_async_copy(arrived, arrived, br_sem.at[row]).wait()
-
-        def predict_rows(tile, carry):
-            at = pl.ds(pl.multiple_of(tile * tall, tall), tall)
-            waves = in_q[row].reshape(devices * parts, channels)
-            after = x[row, at, :].astype(F32) + dot(inv[at, :], waves)
-            second = layer_norm(after, gain2[...][None, :]).astype(BF16)
-            hidden = jax.nn.gelu(dot(second, win[...])).astype(BF16)
-            pred[row, at, :] = (after + dot(hidden, wout[...])).astype(BF16)
-            return carry
-
-        lax.fori_loop(0, length // tall, predict_rows, 0)
-        at_peer = lambda index, peer: pred.at[
-            index, pl.ds(pl.multiple_of(peer * block, block), block), :
-        ]
-        for copy in member_copies(row, at_peer, in_y, ys_sem, yr_sem):
-            copy.start()
-
-    thin = min(32, block)
-
-    def score(row):
-        arrived = in_y.at[row, pl.ds(0, members - 1)]
-        pltpu.make_async_copy(arrived, arrived, yr_sem.at[row]).wait()
-        in_y[row, mine] = pred[row, pl.ds(pl.multiple_of(mine * block, block), block), :]
+            pltpu.make_async_remote_copy(
+                src_ref=pred.at[row, pl.ds(pl.multiple_of(peer * block + half * piece, piece), piece), :],
+                dst_ref=in_y.at[row, half, mine],
+                send_sem=ys_sem.at[row * halves + half],
+                recv_sem=yr_sem.at[row * halves + half],
+                device_id=(peer, me),
+                device_id_type=MESH,
+            ).start()
+
+    def score(row, half):
+        arrived = in_y.at[row, half, pl.ds(0, members - 1)]
+        pltpu.make_async_copy(arrived, arrived, yr_sem.at[row * halves + half]).wait()
+        own = pl.ds(pl.multiple_of(mine * block + half * piece, piece), piece)
+        in_y[row, half, mine] = pred[row, own, :]
 
         def score_rows(tile, carry):
             at = pl.ds(pl.multiple_of(tile * thin, thin), thin)
-            fields = [in_y[row, index, at, :].astype(F32) for index in range(members)]
-            target = obs[row, at, :].astype(F32)
+            fields = [in_y[row, half, index, at, :].astype(F32) for index in range(members)]
+            here = pl.ds(pl.multiple_of(half * piece + tile * thin, thin), thin)
+            target = obs[row, here, :].astype(F32)
             slopes = []
             for index in range(members):
                 gap = fields[index] - target
                 slopes.append(gap * inverse_distance(gap))
-            for first in range(members):
-                for second in range(first + 1, members):
-                    gap = fields[first] - fields[second]
+            for one in range(members):
+                for two in range(one + 1, members):
+                    gap = fields[one] - fields[two]
                     pull = gap * (inverse_distance(gap) * (1.0 / (members - 1)))
-                    slopes[first] = slopes[first] - pull
-                    slopes[second] = slopes[second] + pull
+                    slopes[one] = slopes[one] - pull
+                    slopes[two] = slopes[two] + pull
             for index in range(members):
-                grad[row, index, at, :] = slopes[index].astype(BF16)
-            return carry
-
-        lax.fori_loop(0, block // thin, score_rows, 0)
-        for copy in member_copies(row, lambda index, peer: grad.at[index, peer], in_z, zs_sem, zr_sem):
-            copy.start()
-        in_z[row, mine] = grad[row, mine]
+                grad[row, half, index, at, :] = slopes[index].astype(BF16)
+            return carry
+
+        lax.fori_loop(0, piece // thin, score_rows, 0)
+        there = pl.ds(pl.multiple_of(half * piece, piece), piece)
+        for step in range(1, members):
+            peer = (mine + step) % members
+            pltpu.make_async_remote_copy(
+                src_ref=grad.at[row, half, peer],
+                dst_ref=in_z.at[row, mine, there, :],
+                send_sem=zs_sem.at[row * halves + half],
+                recv_sem=zr_sem.at[row * halves + half],
+                device_id=(peer, me),
+                device_id_type=MESH,
+            ).start()
+        in_z[row, mine, there, :] = grad[row, half, mine]
 
     def finish(row, carry):
-        predict(row)
-
-        @pl.when(row > 0)
-        def _():
-            score(row - 1)
-
+        arrived = in_q.at[row, pl.ds(0, devices - 1)]
+        pltpu.make_async_copy(arrived, arrived, br_sem.at[row]).wait()
+
+        def predict_half(half, inner):
+            predict(row, half)
+            return inner
+
+        def score_half(half, inner):
+            score(row, half)
+            return inner
+
+        lax.fori_loop(0, halves, predict_half, 0)
+        lax.fori_loop(0, halves, score_half, 0)
         return carry
 
     lax.fori_loop(0, rows, finish, 0)
-    score(rows - 1)
-
-    def deliver(row, carry):
-        arrived = in_z.at[row, pl.ds(0, members - 1)]
-        pltpu.make_async_copy(arrived, arrived, zr_sem.at[row]).wait()
+
+    def deliver(index, carry):
+        arrived = in_y.at[0, 0, pl.ds(0, members - 1)]
+        pltpu.make_async_copy(arrived, arrived, zr_sem.at[index]).wait()
+        pltpu.make_async_copy(arrived, arrived, ys_sem.at[index]).wait()
+        pltpu.make_async_copy(arrived, arrived, zs_sem.at[index]).wait()
         return carry
 
-    lax.fori_loop(0, rows, deliver, 0)
-
-    for part in range(2):
-        sent = out_a.at[pl.ds(0, devices - 1), pl.ds(0, half)]
+    lax.fori_loop(0, rows * halves, deliver, 0)
+
+    for part, (lane, width) in enumerate(chunks):
+        sent = out_a.at[pl.ds(0, devices - 1), :, :, pl.ds(lane, width)]
         pltpu.make_async_copy(sent, sent, fs_sem.at[part]).wait()
 
     def drain(row, carry):
         sent = in_q.at[row, pl.ds(0, devices - 1)]
         pltpu.make_async_copy(sent, sent, bs_sem.at[row]).wait()
-        sent = in_y.at[row, pl.ds(0, members - 1)]
-        pltpu.make_async_copy(sent, sent, ys_sem.at[row]).wait()
-        pltpu.make_async_copy(sent, sent, zs_sem.at[row]).wait()
         return carry
 
     lax.fori_loop(0, rows, drain, 0)
@@ -357,6 +381,7 @@
     members = lax.axis_size("member")
     block = length // members
     parts = 2 * slots
+    halves = 2
     forward, inverse = tables(waves, length)
     group = min(8, devices)
     order = group_order(group * rows, parts)
@@ -389,14 +414,14 @@
             pltpu.VMEM(order.shape, BF16),
             pltpu.VMEM((2 * waves, length), BF16),
             pltpu.VMEM((length, 2 * waves), BF16),
-            pltpu.VMEM((length, channels), BF16),
+            pltpu.VMEM((rows, length, channels), BF16),
             pltpu.VMEM((devices, rows, parts, channels), BF16),
             pltpu.VMEM((devices, rows, parts, channels), BF16),
             pltpu.VMEM((parts, lats, channels), BF16),
             pltpu.VMEM((devices, rows, parts, channels), BF16),
             pltpu.VMEM((rows, devices, parts, channels), BF16),
-            pltpu.VMEM((rows, members, block, channels), BF16),
-            pltpu.VMEM((rows, members, block, channels), BF16),
+            pltpu.VMEM((rows, halves, members, block // halves, channels), BF16),
+            pltpu.VMEM((rows, halves, members, block // halves, channels), BF16),
             pltpu.VMEM((waves,), jnp.int32),
             pltpu.SMEM((waves,), jnp.int32),
             pltpu.VMEM((channels,), F32),
@@ -407,10 +432,10 @@
             sems((2,)),
             sems((rows,)),
             sems((rows,)),
-            sems((rows,)),
-            sems((rows,)),
-            sems((rows,)),
-            sems((rows,)),
+            sems((rows * halves,)),
+            sems((rows * halves,)),
+            sems((rows * halves,)),
+            sems((rows * halves,)),
             sems((4,)),
         ],
         compiler_params=pltpu.CompilerParams(

time: 114 us -> 109 us (0.956)
  Pallas kernels: 112 us -> 108 us
    pallas_call x1, Pallas kernels: 110 us -> 106 us  [local(): pl.pallas_call(kernel, out_shape=(pltpu.VMEM((rows, length, channels), BF...]
where the time goes in v3:
time: 109 us; the launch traced here: 108 us
  Pallas kernels  108 us (99%)
    pallas_call x1, Pallas kernels, local(): pl.pallas_call(kernel, out_shape=(pltpu.VMEM((rows, length, channels), BF...  106 us

profile of v3, /device:TPU:2, one launch (start us, length us, event | category | flops | bytes accessed | tf_op | source)
XLA Modules:
  0.0 108.4 jit_solution(6402154183810329208)
XLA Ops:
  0.6 106.1 %shard_map.140 = (bf16[4,512,384]{2,1,0:T(8,128)(2,1)S(1)}, bf16[4,4,128,384]{3,2,1,0:T(8,128)(2,1)S(1)}) custom-call(bf16[1,4,512,384]{3,2,1,0:T(8,128)(2,1)} %x_hbm.1, bf16[4,512,384]{2,1,0:T(8,128)(2,1)} %obs_hbm.1, s32[256]{0:T(256)} %slot_hbm.1, bf16[4,256,256]{2,1,0:T(8,128)(2,1)} %legf_hbm.1, bf16[4,256,256]{2,1,0:T(8,128)(2,1)} %legi_hbm.1, ...), custom_call_target="tpu_custom_call" | custom-call | tf_op jit(solution)/shard_map/pallas_call | solution.py:396
  106.7 1.7 %shard_map.141 = (bf16[1,4,512,384]{3,2,1,0:T(8,128)(2,1)}, bf16[1,4,512,384]{3,2,1,0:T(8,128)(2,1)}) custom-call(bf16[4,512,384]{2,1,0:T(8,128)(2,1)S(1)} %get-tuple-element.4.pred, bf16[4,512,384]{2,1,0:T(8,128)(2,1)S(1)} %bitcast.1), custom_call_target="tpu_custom_call" | custom-call | tf_op jit(solution)/shard_map/pallas_call | solution.py:448

commit v4 on v3

--- a/solution.py
+++ b/solution.py
@@ -79,7 +79,8 @@
         pl.semaphore_signal(barrier, inc=1, device_id=(mine, lat_peer(step)), device_id_type=MESH)
         return carry
 
-    lax.fori_loop(1, devices, greet, 0)
+    lax.fori_loop(devices // 2, devices, greet, 0)
+    lax.fori_loop(1, devices // 2, greet, 0)
     for step in range(1, members):
         pl.semaphore_signal(
             barrier, inc=1, device_id=((mine + step) % members, me), device_id_type=MESH
@@ -140,28 +141,27 @@
 
         return lax.fori_loop(0, length // wide, norm_tile, carry)
 
-    wide = min(128, length)
-    for row in range(rows):
-        x_loads[row].wait()
-        norm_rows(row, 0)
-
-    for part, (lane, width) in enumerate(chunks):
+    wide = min(256, length)
+
+    def analyse_and_send(start, count, part):
+        lane, width = chunks[part]
         lanes = pl.ds(lane, width)
+        these = pl.ds(start, count)
 
         def analyse(row, carry):
             found = dot(fwd[...], normed[row, :, lanes]).astype(BF16)
             out_a[:, row, :, lanes] = found.reshape(devices, parts, width)
             return carry
 
-        lax.fori_loop(0, rows, analyse, 0)
-        if part == 0:
+        lax.fori_loop(start, start + count, analyse, 0)
+        if start == 0 and part == 0:
             pl.semaphore_wait(barrier, devices - 1 + members - 1)
 
         def send(step, carry):
             peer = lat_peer(step)
             pltpu.make_async_remote_copy(
-                src_ref=out_a.at[peer, :, :, lanes],
-                dst_ref=in_r.at[me, :, :, lanes],
+                src_ref=out_a.at[peer, these, :, lanes],
+                dst_ref=in_r.at[me, these, :, lanes],
                 send_sem=fs_sem.at[part],
                 recv_sem=fr_sem.at[part],
                 device_id=(mine, peer),
@@ -170,6 +170,14 @@
             return carry
 
         lax.fori_loop(1, devices, send, 0)
+
+    pair = rows // 2
+    for start in range(0, rows, pair):
+        for row in range(start, start + pair):
+            x_loads[row].wait()
+        lax.fori_loop(start, start + pair, norm_rows, 0)
+        analyse_and_send(start, pair, 0)
+    analyse_and_send(0, rows, 1)
     in_r[me] = out_a[me]
 
     loads[1].wait()

time: 109 us -> 108 us (level)
  no operation moved by 1% of the time
where the time goes in v4:
time: 108 us; the launch traced here: 107 us
  Pallas kernels  107 us (99%)
    pallas_call x1, Pallas kernels, local(): pl.pallas_call(kernel, out_shape=(pltpu.VMEM((rows, length, channels), BF...  105 us

profile of v4, /device:TPU:2, one launch (start us, length us, event | category | flops | bytes accessed | tf_op | source)
XLA Modules:
  0.0 107.5 jit_solution(14826022856674544148)
XLA Ops:
  0.6 105.2 %shard_map.140 = (bf16[4,512,384]{2,1,0:T(8,128)(2,1)S(1)}, bf16[4,4,128,384]{3,2,1,0:T(8,128)(2,1)S(1)}) custom-call(bf16[1,4,512,384]{3,2,1,0:T(8,128)(2,1)} %x_hbm.1, bf16[4,512,384]{2,1,0:T(8,128)(2,1)} %obs_hbm.1, s32[256]{0:T(256)} %slot_hbm.1, bf16[4,256,256]{2,1,0:T(8,128)(2,1)} %legf_hbm.1, bf16[4,256,256]{2,1,0:T(8,128)(2,1)} %legi_hbm.1, ...), custom_call_target="tpu_custom_call" | custom-call | tf_op jit(solution)/shard_map/pallas_call | solution.py:404
  105.8 1.7 %shard_map.141 = (bf16[1,4,512,384]{3,2,1,0:T(8,128)(2,1)}, bf16[1,4,512,384]{3,2,1,0:T(8,128)(2,1)}) custom-call(bf16[4,512,384]{2,1,0:T(8,128)(2,1)S(1)} %get-tuple-element.4.pred, bf16[4,512,384]{2,1,0:T(8,128)(2,1)S(1)} %bitcast.1), custom_call_target="tpu_custom_call" | custom-call | tf_op jit(solution)/shard_map/pallas_call | solution.py:456

commit v5 on v3

--- a/solution.py
+++ b/solution.py
@@ -46,6 +46,10 @@
     return lax.rsqrt(jnp.mean(jnp.square(difference), -1, keepdims=True) + EPS_DIST)
 
 
+def first_lanes(channels):
+    return 2 * channels // 3 // 128 * 128
+
+
 def dot(a, b):
     return jnp.dot(a, b, preferred_element_type=F32)
 
@@ -55,7 +59,7 @@
     cf_hbm, ci_hbm, order_hbm,
     pred, in_z,
     x, obs, legf, legi, filt, win, wout, cf, ci, order,
-    fwd, inv, normed, out_a, in_r, spec, out_b, in_q, in_y, grad,
+    fwd, inv, normed, out_a0, out_a1, in_r0, in_r1, spec, out_b, in_q, in_y, grad,
     slot_ref, slot_smem, gain1, gain2,
     load_sem, x_sem, fs_sem, fr_sem, bs_sem, br_sem, ys_sem, yr_sem, zs_sem, zr_sem, small_sem,
 ):
@@ -65,25 +69,14 @@
     mine = lax.axis_index("member")
     rows, length, channels = x.shape
     degrees = legf.shape[1]
-    parts = out_a.shape[2]
+    parts = out_a0.shape[2]
+    outs_a, ins_r = [out_a0, out_a1], [in_r0, in_r1]
     slots = parts // 2
     block = length // members
     stride = 1
 
     def lat_peer(step):
         return (me + stride * step) % devices
-
-    barrier = pltpu.get_barrier_semaphore()
-
-    def greet(step, carry):
-        pl.semaphore_signal(barrier, inc=1, device_id=(mine, lat_peer(step)), device_id_type=MESH)
-        return carry
-
-    lax.fori_loop(1, devices, greet, 0)
-    for step in range(1, members):
-        pl.semaphore_signal(
-            barrier, inc=1, device_id=((mine + step) % members, me), device_id_type=MESH
-        )
 
     x_loads = [
         pltpu.make_async_copy(x_hbm.at[0, row], x.at[row], x_sem.at[row]) for row in range(rows)
@@ -114,6 +107,19 @@
         load.start()
     obs_load.start()
 
+    barrier = pltpu.get_barrier_semaphore()
+
+    def greet(step, carry):
+        pl.semaphore_signal(barrier, inc=1, device_id=(mine, lat_peer(step)), device_id_type=MESH)
+        return carry
+
+    lax.fori_loop(devices // 2, devices, greet, 0)
+    lax.fori_loop(1, devices // 2, greet, 0)
+    for step in range(1, members):
+        pl.semaphore_signal(
+            barrier, inc=1, device_id=((mine + step) % members, me), device_id_type=MESH
+        )
+
     for load in small:
         load.wait()
     spread = (degrees, 2 * degrees)
@@ -129,7 +135,7 @@
         picked, cf[...], (((0,), (0,)), ((), ())), preferred_element_type=F32
     ).astype(BF16)
 
-    first = 2 * channels // 3 // 128 * 128
+    first = first_lanes(channels)
     chunks = [(0, first), (first, channels - first)]
 
     def norm_rows(row, carry):
@@ -140,17 +146,19 @@
 
         return lax.fori_loop(0, length // wide, norm_tile, carry)
 
-    wide = min(128, length)
+    wide = min(256, length)
+
     for row in range(rows):
         x_loads[row].wait()
         norm_rows(row, 0)
 
     for part, (lane, width) in enumerate(chunks):
         lanes = pl.ds(lane, width)
+        out_a, in_r = outs_a[part], ins_r[part]
 
         def analyse(row, carry):
             found = dot(fwd[...], normed[row, :, lanes]).astype(BF16)
-            out_a[:, row, :, lanes] = found.reshape(devices, parts, width)
+            out_a[:, row] = found.reshape(devices, parts, width)
             return carry
 
         lax.fori_loop(0, rows, analyse, 0)
@@ -160,8 +168,8 @@
         def send(step, carry):
             peer = lat_peer(step)
             pltpu.make_async_remote_copy(
-                src_ref=out_a.at[peer, :, :, lanes],
-                dst_ref=in_r.at[me, :, :, lanes],
+                src_ref=out_a.at[peer],
+                dst_ref=in_r.at[me],
                 send_sem=fs_sem.at[part],
                 recv_sem=fr_sem.at[part],
                 device_id=(mine, peer),
@@ -170,7 +178,7 @@
             return carry
 
         lax.fori_loop(1, devices, send, 0)
-    in_r[me] = out_a[me]
+        in_r[me] = out_a[me]
 
     loads[1].wait()
     inv[...] = dot(ci[...], picked).astype(BF16)
@@ -202,11 +210,12 @@
 
     for part, (lane, width) in enumerate(chunks):
         lanes = pl.ds(lane, width)
-        everything = in_r.at[pl.ds(0, devices - 1), :, :, lanes]
+        in_r = ins_r[part]
+        everything = in_r.at[pl.ds(0, devices - 1)]
         pltpu.make_async_copy(everything, everything, fr_sem.at[part]).wait()
 
         def gather(index, carry):
-            taken = in_r[pl.ds(index * group, group), :, :, lanes].reshape(points * parts, width)
+            taken = in_r[pl.ds(index * group, group)].reshape(points * parts, width)
             moved = dot(order[...], taken).astype(BF16)
             at = pl.ds(pl.multiple_of(index * points, points), points)
             spec[:, at, lanes] = moved.reshape(parts, points, width)
@@ -347,7 +356,7 @@
     lax.fori_loop(0, rows * halves, deliver, 0)
 
     for part, (lane, width) in enumerate(chunks):
-        sent = out_a.at[pl.ds(0, devices - 1), :, :, pl.ds(lane, width)]
+        sent = outs_a[part].at[pl.ds(0, devices - 1)]
         pltpu.make_async_copy(sent, sent, fs_sem.at[part]).wait()
 
     def drain(row, carry):
@@ -382,6 +391,7 @@
     block = length // members
     parts = 2 * slots
     halves = 2
+    first = first_lanes(channels)
     forward, inverse = tables(waves, length)
     group = min(8, devices)
     order = group_order(group * rows, parts)
@@ -415,8 +425,10 @@
             pltpu.VMEM((2 * waves, length), BF16),
             pltpu.VMEM((length, 2 * waves), BF16),
             pltpu.VMEM((rows, length, channels), BF16),
-            pltpu.VMEM((devices, rows, parts, channels), BF16),
-            pltpu.VMEM((devices, rows, parts, channels), BF16),
+            pltpu.VMEM((devices, rows, parts, first), BF16),
+            pltpu.VMEM((devices, rows, parts, channels - first), BF16),
+            pltpu.VMEM((devices, rows, parts, first), BF16),
+            pltpu.VMEM((devices, rows, parts, channels - first), BF16),
             pltpu.VMEM((parts, lats, channels), BF16),
             pltpu.VMEM((devices, rows, parts, channels), BF16),
             pltpu.VMEM((rows, devices, parts, channels), BF16),

time: 109 us -> 108 us (level)
  no operation moved by 1% of the time
where the time goes in v5:
time: 108 us
  Pallas kernels  107 us (99%)
    pallas_call x1, Pallas kernels, local(): pl.pallas_call(kernel, out_shape=(pltpu.VMEM((rows, length, channels), BF...  106 us

profile of v5, /device:TPU:2, one launch (start us, length us, event | category | flops | bytes accessed | tf_op | source)
XLA Modules:
  0.0 108.0 jit_solution(1746474245750129499)
XLA Ops:
  0.6 105.7 %shard_map.140 = (bf16[4,512,384]{2,1,0:T(8,128)(2,1)S(1)}, bf16[4,4,128,384]{3,2,1,0:T(8,128)(2,1)S(1)}) custom-call(bf16[1,4,512,384]{3,2,1,0:T(8,128)(2,1)} %x_hbm.1, bf16[4,512,384]{2,1,0:T(8,128)(2,1)} %obs_hbm.1, s32[256]{0:T(256)} %slot_hbm.1, bf16[4,256,256]{2,1,0:T(8,128)(2,1)} %legf_hbm.1, bf16[4,256,256]{2,1,0:T(8,128)(2,1)} %legi_hbm.1, ...), custom_call_target="tpu_custom_call" | custom-call | tf_op jit(solution)/shard_map/pallas_call | solution.py:406
  106.4 1.7 %shard_map.141 = (bf16[1,4,512,384]{3,2,1,0:T(8,128)(2,1)}, bf16[1,4,512,384]{3,2,1,0:T(8,128)(2,1)}) custom-call(bf16[4,512,384]{2,1,0:T(8,128)(2,1)S(1)} %get-tuple-element.4.pred, bf16[4,512,384]{2,1,0:T(8,128)(2,1)S(1)} %bitcast.1), custom_call_target="tpu_custom_call" | custom-call | tf_op jit(solution)/shard_map/pallas_call | solution.py:460

commit v6 on v5

--- a/solution.py
+++ b/solution.py
@@ -249,11 +249,9 @@
 
     everywhere = pl.ds(0, channels)
 
-    def send_rest(row, carry):
+    ahead = min(2, rows)
+    for row in range(1, ahead):
         send_back(row, everywhere)
-        return carry
-
-    lax.fori_loop(1, rows, send_rest, 0)
     for row in range(rows):
         in_q[row, me] = out_b[me, row]
     obs_load.wait()
@@ -328,6 +326,10 @@
             ).start()
         in_z[row, mine, there, :] = grad[row, half, mine]
 
+    def wait_sent(row):
+        sent = in_q.at[row, pl.ds(0, devices - 1)]
+        pltpu.make_async_copy(sent, sent, bs_sem.at[row]).wait()
+
     def finish(row, carry):
         arrived = in_q.at[row, pl.ds(0, devices - 1)]
         pltpu.make_async_copy(arrived, arrived, br_sem.at[row]).wait()
@@ -341,6 +343,12 @@
             return inner
 
         lax.fori_loop(0, halves, predict_half, 0)
+
+        @pl.when(row + ahead < rows)
+        def _():
+            wait_sent(row)
+            send_back(row + ahead, everywhere)
+
         lax.fori_loop(0, halves, score_half, 0)
         return carry
 
@@ -360,11 +368,10 @@
         pltpu.make_async_copy(sent, sent, fs_sem.at[part]).wait()
 
     def drain(row, carry):
-        sent = in_q.at[row, pl.ds(0, devices - 1)]
-        pltpu.make_async_copy(sent, sent, bs_sem.at[row]).wait()
+        wait_sent(row)
         return carry
 
-    lax.fori_loop(0, rows, drain, 0)
+    lax.fori_loop(rows - ahead, rows, drain, 0)
 
 
 def store(pred, slope, pred_out, slope_out, sem):

time: 108 us -> 108 us (level)
  no operation moved by 1% of the time
where the time goes in v6:
time: 108 us
  Pallas kernels  107 us (99%)
    pallas_call x1, Pallas kernels, local(): pl.pallas_call(kernel, out_shape=(pltpu.VMEM((rows, length, channels), BF...  106 us

profile of v6, /device:TPU:2, one launch (start us, length us, event | category | flops | bytes accessed | tf_op | source)
XLA Modules:
  0.0 108.0 jit_solution(9510262840683988733)
XLA Ops:
  0.6 105.7 %shard_map.140 = (bf16[4,512,384]{2,1,0:T(8,128)(2,1)S(1)}, bf16[4,4,128,384]{3,2,1,0:T(8,128)(2,1)S(1)}) custom-call(bf16[1,4,512,384]{3,2,1,0:T(8,128)(2,1)} %x_hbm.1, bf16[4,512,384]{2,1,0:T(8,128)(2,1)} %obs_hbm.1, s32[256]{0:T(256)} %slot_hbm.1, bf16[4,256,256]{2,1,0:T(8,128)(2,1)} %legf_hbm.1, bf16[4,256,256]{2,1,0:T(8,128)(2,1)} %legi_hbm.1, ...), custom_call_target="tpu_custom_call" | custom-call | tf_op jit(solution)/shard_map/pallas_call | solution.py:413
  106.4 1.7 %shard_map.141 = (bf16[1,4,512,384]{3,2,1,0:T(8,128)(2,1)}, bf16[1,4,512,384]{3,2,1,0:T(8,128)(2,1)}) custom-call(bf16[4,512,384]{2,1,0:T(8,128)(2,1)S(1)} %get-tuple-element.4.pred, bf16[4,512,384]{2,1,0:T(8,128)(2,1)S(1)} %bitcast.1), custom_call_target="tpu_custom_call" | custom-call | tf_op jit(solution)/shard_map/pallas_call | solution.py:467

commit v7 on v5

--- a/solution.py
+++ b/solution.py
@@ -148,28 +148,31 @@
 
     wide = min(256, length)
 
-    for row in range(rows):
-        x_loads[row].wait()
-        norm_rows(row, 0)
-
-    for part, (lane, width) in enumerate(chunks):
-        lanes = pl.ds(lane, width)
+    pair = rows // 2
+    steps = [(0, pair, 0), (pair, pair, 0), (0, rows, 1)]
+    for start, count, part in steps:
+        lane, width = chunks[part]
+        lanes, these = pl.ds(lane, width), pl.ds(start, count)
         out_a, in_r = outs_a[part], ins_r[part]
+        if part == 0:
+            for row in range(start, start + count):
+                x_loads[row].wait()
+            lax.fori_loop(start, start + count, norm_rows, 0)
 
         def analyse(row, carry):
             found = dot(fwd[...], normed[row, :, lanes]).astype(BF16)
             out_a[:, row] = found.reshape(devices, parts, width)
             return carry
 
-        lax.fori_loop(0, rows, analyse, 0)
-        if part == 0:
+        lax.fori_loop(start, start + count, analyse, 0)
+        if start == 0 and part == 0:
             pl.semaphore_wait(barrier, devices - 1 + members - 1)
 
         def send(step, carry):
             peer = lat_peer(step)
             pltpu.make_async_remote_copy(
-                src_ref=out_a.at[peer],
-                dst_ref=in_r.at[me],
+                src_ref=out_a.at[peer, these],
+                dst_ref=in_r.at[me, these],
                 send_sem=fs_sem.at[part],
                 recv_sem=fr_sem.at[part],
                 device_id=(mine, peer),
@@ -178,7 +181,8 @@
             return carry
 
         lax.fori_loop(1, devices, send, 0)
-        in_r[me] = out_a[me]
+    for part in range(2):
+        ins_r[part][me] = outs_a[part][me]
 
     loads[1].wait()
     inv[...] = dot(ci[...], picked).astype(BF16)
@@ -390,7 +394,7 @@
     members = lax.axis_size("member")
     block = length // members
     parts = 2 * slots
-    halves = 2
+    halves = 4
     first = first_lanes(channels)
     forward, inverse = tables(waves, length)
     group = min(8, devices)

time: 108 us -> 104 us (0.963)
  Pallas kernels: 107 us -> 103 us
    pallas_call x1, Pallas kernels: 106 us -> 101 us  [local(): pl.pallas_call(kernel, out_shape=(pltpu.VMEM((rows, length, channels), BF...]
where the time goes in v7:
time: 104 us
  Pallas kernels  103 us (99%)
    pallas_call x1, Pallas kernels, local(): pl.pallas_call(kernel, out_shape=(pltpu.VMEM((rows, length, channels), BF...  101 us

profile of v7, /device:TPU:2, one launch (start us, length us, event | category | flops | bytes accessed | tf_op | source)
XLA Modules:
  0.0 103.8 jit_solution(13253743594955953732)
XLA Ops:
  0.6 101.5 %shard_map.140 = (bf16[4,512,384]{2,1,0:T(8,128)(2,1)S(1)}, bf16[4,4,128,384]{3,2,1,0:T(8,128)(2,1)S(1)}) custom-call(bf16[1,4,512,384]{3,2,1,0:T(8,128)(2,1)} %x_hbm.1, bf16[4,512,384]{2,1,0:T(8,128)(2,1)} %obs_hbm.1, s32[256]{0:T(256)} %slot_hbm.1, bf16[4,256,256]{2,1,0:T(8,128)(2,1)} %legf_hbm.1, bf16[4,256,256]{2,1,0:T(8,128)(2,1)} %legi_hbm.1, ...), custom_call_target="tpu_custom_call" | custom-call | tf_op jit(solution)/shard_map/pallas_call | solution.py:410
  102.1 1.7 %shard_map.141 = (bf16[1,4,512,384]{3,2,1,0:T(8,128)(2,1)}, bf16[1,4,512,384]{3,2,1,0:T(8,128)(2,1)}) custom-call(bf16[4,512,384]{2,1,0:T(8,128)(2,1)S(1)} %get-tuple-element.4.pred, bf16[4,512,384]{2,1,0:T(8,128)(2,1)S(1)} %bitcast.1), custom_call_target="tpu_custom_call" | custom-call | tf_op jit(solution)/shard_map/pallas_call | solution.py:464

commit v8 on v7

--- a/solution.py
+++ b/solution.py
@@ -394,7 +394,7 @@
     members = lax.axis_size("member")
     block = length // members
     parts = 2 * slots
-    halves = 4
+    halves = 8
     first = first_lanes(channels)
     forward, inverse = tables(waves, length)
     group = min(8, devices)

time: 104 us -> 109 us (1.048)
  Pallas kernels: 103 us -> 109 us
    pallas_call x1, Pallas kernels: 101 us -> 107 us  [local(): pl.pallas_call(kernel, out_shape=(pltpu.VMEM((rows, length, channels), BF...]
where the time goes in v8:
time: 109 us
  Pallas kernels  109 us (100%)
    pallas_call x1, Pallas kernels, local(): pl.pallas_call(kernel, out_shape=(pltpu.VMEM((rows, length, channels), BF...  107 us

profile of v8, /device:TPU:2, one launch (start us, length us, event | category | flops | bytes accessed | tf_op | source)
XLA Modules:
  0.0 109.2 jit_solution(11057378399333780341)
XLA Ops:
  0.6 106.9 %shard_map.140 = (bf16[4,512,384]{2,1,0:T(8,128)(2,1)S(1)}, bf16[4,4,128,384]{3,2,1,0:T(8,128)(2,1)S(1)}) custom-call(bf16[1,4,512,384]{3,2,1,0:T(8,128)(2,1)} %x_hbm.1, bf16[4,512,384]{2,1,0:T(8,128)(2,1)} %obs_hbm.1, s32[256]{0:T(256)} %slot_hbm.1, bf16[4,256,256]{2,1,0:T(8,128)(2,1)} %legf_hbm.1, bf16[4,256,256]{2,1,0:T(8,128)(2,1)} %legi_hbm.1, ...), custom_call_target="tpu_custom_call" | custom-call | tf_op jit(solution)/shard_map/pallas_call | solution.py:410
  107.5 1.7 %shard_map.141 = (bf16[1,4,512,384]{3,2,1,0:T(8,128)(2,1)}, bf16[1,4,512,384]{3,2,1,0:T(8,128)(2,1)}) custom-call(bf16[4,512,384]{2,1,0:T(8,128)(2,1)S(1)} %get-tuple-element.4.pred, bf16[4,512,384]{2,1,0:T(8,128)(2,1)S(1)} %bitcast.1), custom_call_target="tpu_custom_call" | custom-call | tf_op jit(solution)/shard_map/pallas_call | solution.py:464
